TPU v7x, 32 devices: a whole 2x2x4 slice. The times are simulated.
32 devices in a mesh: sample: 2 (over y), gz: 4 (over x, core), gy: 4 (over z).
Axes of the slice: x: 2, y: 2, z: 4, core: 2. Of those that a mesh axis runs over, the one named last changes fastest.
Arguments:
- right_side: float32 [64, 64, 256], P(('sample', 'gz'), 'gy'), parts along dimension 0, may hold values from -8 to 8
- labels: int32 [8, 8, 32], P(('sample', 'gz'), 'gy'), parts along dimension 0, may hold values from 0 to 7
- region_coeff: float32 [16], P('sample'), parts along dimension 0, may hold values from 0.2 to 5
- shift_index: int32 [16], P('sample'), parts along dimension 0, may hold values from 0 to 15
- shift_table: float32 [16], replicated, may hold values from 0.1 to 4
- time_step: float32 [2], P('sample'), parts along dimension 0, may hold values from 0.3 to 1
- block_inverse: float32 [8, 128, 128], replicated, as said below
Outputs:
- solution: float32 [8, 64, 64, 256], P(None, ('sample', 'gz'), 'gy'), parts along dimension 1
- residual: float32 [8, 64, 64, 256], P(None, ('sample', 'gz'), 'gy'), parts along dimension 1
There are 2 independent parts, one for each index of `sample`. A program takes and returns all parts, laid end to end along the dimension named above; an argument that names none is the same for every part. Nothing has to cross between parts.
Inputs may be any that keep to these rules, and one draw needn't show every extreme that they name: `shift_index`: a table row for each system. `labels`: a region for each block. `block_inverse`: each block is symmetric and positive definite.
All inputs are finite; a program needn't handle non-finite values.
Results may differ from a plain program's by a relative error of at most 0.00022.
Values sent between devices are 32-bit elements; how exact they have to be, the bound alone decides.
A program may use at most 64 MiB of HBM per device.

v0:
```python
import jax
import jax.numpy as jnp
from jax import lax
from jax.sharding import PartitionSpec as P

SHIFTS = 8
ITERS = 2
BLOCK = 128


NEIGHBOURS = [
    (step_z, step_y, step_x, 0.5 ** (abs(step_z) + abs(step_y) + abs(step_x) - 1))
    for step_z in (-1, 0, 1)
    for step_y in (-1, 0, 1)
    for step_x in (-1, 0, 1)
    if (step_z, step_y, step_x) != (0, 0, 0)
]


def padded_2(block, sides, width):
    for axis, dim in sides:
        count = lax.axis_size(axis)
        forward = [(i, i + 1) for i in range(count - 1)]
        backward = [(target, source) for source, target in forward]
        low = lax.ppermute(
            lax.slice_in_dim(block, block.shape[dim] - width, None, axis=dim), axis, forward
        )
        high = lax.ppermute(lax.slice_in_dim(block, 0, width, axis=dim), axis, backward)
        block = jnp.concatenate([low, block, high], axis=dim)
    return block


def cell_values(labels, region_coeff):
    picked = jnp.where(labels[..., None] == jnp.arange(region_coeff.shape[0]), region_coeff, 0.0)
    table = jnp.sum(picked, axis=-1)
    return jnp.repeat(jnp.repeat(jnp.repeat(table, 8, 0), 8, 1), 8, 2)


def stencil(field, padded, conductivity, padded_cond):
    depth, rows, width = (field.shape[-3], field.shape[-2], field.shape[-1])
    total = jnp.zeros_like(field)
    for step_z, step_y, step_x, weight in NEIGHBOURS:
        beside = padded[
            ...,
            1 + step_z : 1 + step_z + depth,
            1 + step_y : 1 + step_y + rows,
            1 + step_x : 1 + step_x + width,
        ]
        cond_beside = padded_cond[
            1 + step_z : 1 + step_z + depth,
            1 + step_y : 1 + step_y + rows,
            1 + step_x : 1 + step_x + width,
        ]
        total = total + weight * 0.5 * (conductivity + cond_beside) * (field - beside)
    return total


def extend_field(field):
    extended = padded_2(field, (("gz", 1), ("gy", 2)), 1)
    return jnp.pad(extended, ((0, 0), (0, 0), (0, 0), (1, 1)))


def global_sum(values):
    row_sum = lax.psum(values, "gy")
    return lax.psum(row_sum, "gz")


def precondition(residual, block_inverse):
    shape = residual.shape
    blocks = residual.reshape(shape[0], shape[1], shape[2], shape[3] // BLOCK, BLOCK)
    result = jnp.einsum("szyxb,sbc->szyxc", blocks, block_inverse, precision=lax.Precision.HIGHEST)
    return result.reshape(shape)


def per_system(values):
    return values.reshape(values.shape[0], 1, 1, 1)


def on_device(right_side, labels, region_coeff, shift_index, shift_table, time_step, block_inverse):
    conductivity = cell_values(labels, region_coeff)
    cond_rim = padded_2(conductivity, (("gz", 0), ("gy", 1)), 1)
    padded_cond = jnp.pad(cond_rim, ((0, 0), (0, 0), (1, 1)))
    shift_values = jnp.sum(
        jnp.where(shift_index[:, None] == jnp.arange(shift_table.shape[0]), shift_table, 0.0),
        axis=1,
    )
    scale = time_step[0]
    residual = jnp.broadcast_to(right_side[None], (SHIFTS,) + right_side.shape)
    solution = jnp.zeros_like(residual)
    precond = precondition(residual, block_inverse)
    direction = precond
    rz_now = global_sum(jnp.sum(residual * precond, axis=(1, 2, 3)))
    for iteration in range(ITERS):
        padded = extend_field(direction)
        image = per_system(shift_values) * direction + scale * stencil(
            direction, padded, conductivity, padded_cond
        )
        curvature = global_sum(jnp.sum(direction * image, axis=(1, 2, 3)))
        alpha = per_system(rz_now / curvature)
        solution = solution + alpha * direction
        residual = residual - alpha * image
        precond = precondition(residual, block_inverse)
        rz_next = global_sum(jnp.sum(residual * precond, axis=(1, 2, 3)))
        direction = precond + per_system(rz_next / rz_now) * direction
        rz_now = rz_next
    return (solution, residual)


def solution(mesh):
    in_specs = (
        P(("sample", "gz"), "gy", None),
        P(("sample", "gz"), "gy", None),
        P("sample"),
        P("sample"),
        P(),
        P("sample"),
        P(),
    )
    out_specs = (P(None, ("sample", "gz"), "gy", None), P(None, ("sample", "gz"), "gy", None))
    return jax.shard_map(
        on_device, mesh=mesh, in_specs=in_specs, out_specs=out_specs, check_vma=False
    )
```

profile of v0, /device:TPU:0, one launch (start us, length us, event | category | flops | bytes accessed | tf_op | source)
XLA Modules:
  0.0 131.5 jit_solution(17609959154963669425)
XLA Ops:
  0.7 0.8 select_reduce_fusion
  1.5 0.1 copy.32
  1.6 1.3 collective-permute-start.1
  2.9 3.0 %collective-permute-start = (f32[1,16,256]{1,2,0:T(8,128)S(1)}, f32[1,16,256]{1,2,0:T(8,128)S(1)}, u32[]{:S(2)}, u32[]{:S(2)}) collective-permute-start(f32[1,16,256]{1,2,0:T(8,128)S(1)} %get-tuple-element.54), channel_id=1, source_target_pairs={{0,4},{4,8},{8,12},{1,5},{5,9},{9,13},{2,6},{6,10},{10,14},{3,7},{... | collective-permute-start | bytes 49160 | tf_op jit(solution)/shard_map/ppermute | solution.py:25
  6.0 0.9 copy_bitcast_fusion.1
  6.9 1.1 multiply_reduce_fusion.2
  8.0 1.0 copy-done.4
  9.0 1.3 collective-permute-start.5
  10.3 5.1 %collective-permute-start.4 = (f32[8,1,16,256]{3,2,1,0:T(8,128)S(1)}, f32[8,1,16,256]{3,2,1,0:T(8,128)S(1)}, u32[]{:S(2)}, u32[]{:S(2)}) collective-permute-start(f32[8,1,16,256]{3,2,1,0:T(8,128)S(1)} %get-tuple-element.19), channel_id=1, source_target_pairs={{0,4},{4,8},{8,12},{1,5},{5,9},{9,13},{2,6},{6,10},{10,14},{3,7},{... | collective-permute-start | bytes 393224 | tf_op jit(solution)/shard_map/ppermute | solution.py:25
  15.5 0.2 select_reduce_fusion.1
  16.4 0.1 copy.35
  16.5 0.1 copy.34
  16.6 3.5 %collective-permute-start.2 = (f32[10,1,256]{2,1,0:T(1,128)S(1)}, f32[10,1,256]{2,1,0:T(1,128)S(1)}, u32[]{:S(2)}, u32[]{:S(2)}) collective-permute-start(f32[10,1,256]{2,1,0:T(1,128)S(1)} %get-tuple-element.46), channel_id=1, source_target_pairs={{0,1},{1,2},{2,3},{4,5},{5,6},{6,7},{8,9},{9,10},{10,11},{12,13},{... | collective-permute-start | bytes 30728 | tf_op jit(solution)/shard_map/ppermute | solution.py:25
  20.1 1.3 collective-permute-start.3
  21.4 0.8 fusion.153
  22.1 3.5 %collective-permute-done.3 = f32[10,1,256]{2,1,0:T(1,128)S(1)} collective-permute-done((f32[10,1,256]{2,1,0:T(1,128)S(1)}, f32[10,1,256]{2,1,0:T(1,128)S(1)}, u32[]{:S(2)}, u32[]{:S(2)}) %collective-permute-start.3) | collective-permute-done | bytes 10272 | tf_op jit(solution)/shard_map/ppermute | solution.py:28
  25.6 0.2 select_maximum_fusion.6
  25.9 1.5 %fusion.157 = (f32[8,16,256]{2,1,0:T(8,128)S(1)}, f32[8,16,256]{2,1,0:T(8,128)S(1)}, f32[8,16,256]{2,1,0:T(8,128)S(1)}, f32[8,16,256]{2,1,0:T(8,128)S(1)}, f32[8...) fusion(f32[10,18,258]{2,1,0:T(8,128)S(1)} %select_maximum_fusio, ...), kind=kLoop, calls=%fused_computation.268 | loop fusion | flops 1179648 | bytes 4734976 | tf_op jit(solution)/shard_map/mul | solution.py:54
  27.5 0.1 constant_dynamic-update-slice_fusion.1
  27.6 0.1 fusion.160
  27.7 3.5 %collective-permute-start.6 = (f32[8,10,1,256]{3,2,1,0:T(1,128)S(1)}, f32[8,10,1,256]{3,2,1,0:T(1,128)S(1)}, u32[]{:S(2)}, u32[]{:S(2)}) collective-permute-start(f32[8,10,1,256]{3,2,1,0:T(1,128)S(1)} %get-tuple-element.14), channel_id=1, source_target_pairs={{0,1},{1,2},{2,3},{4,5},{5,6},{6,7},{8,9},{9,10},{10,11},{12,13},{... | collective-permute-start | bytes 245768 | tf_op jit(solution)/shard_map/ppermute | solution.py:25
  31.2 1.3 collective-permute-start.7
  32.5 0.9 fusion.156
  33.4 4.1 %collective-permute-done.7 = f32[8,10,1,256]{3,2,1,0:T(1,128)S(1)} collective-permute-done((f32[8,10,1,256]{3,2,1,0:T(1,128)S(1)}, f32[8,10,1,256]{3,2,1,0:T(1,128)S(1)}, u32[]{:S(2)}, u32[]{:S(2)}) %collective-permute-start.7) | collective-permute-done | bytes 81952 | tf_op jit(solution)/shard_map/ppermute | solution.py:28
  37.6 1.5 %select_maximum_fusion.4 = f32[8,10,18,258]{3,2,1,0:T(8,128)S(1)} fusion(f32[8,10,1,256]{3,2,1,0:T(1,128)S(1)} %collective-permute-done.7, f32[8,10,16,256]{3,2,1,0:T(8,128)S(1)} %constant_dynamic-update-slice_fusion, f32[8,10,1,256]{3,2,1,0:T(1,128)S(1)} %collective-permute-done.6), kind=kLoop, calls=%fused_computation.6 | loop fusion | flops 2972160 | bytes 2960640 | tf_op jit(solution)/shard_map/concatenate | solution.py:29
  39.1 9.8 %multiply_reduce_fusion.1 = (f32[8]{0:T(128)S(1)}, f32[8,8,16,256]{3,2,1,0:T(8,128)S(1)}) fusion(f32[8,8,16,256]{3,2,1,0:T(8,128)} %copy-done.4, f32[8,10,18,258]{3,2,1,0:T(8,128)S(1)} %select_maximum_fusion.4, f32[8,16,256]{2,1,0:T(8,128)} %get-tuple-element.37, f32[8,10,1,256]{3,2,1,0:T(1,128)} %copy-done.10, f32[8,10,16,256]{3,2,1,0:T(8,128)} %copy-done.3, ...), kind=kLoop, calls=%fused_computation.198 | loop fusion | flops 23592952 | bytes 27164740 | tf_op jit(solution)/shard_map/reduce_sum | solution.py:98
  49.0 9.9 %all-reduce.3 = (f32[8]{0:T(128)S(1)}, f32[8]{0:T(128)S(1)}) all-reduce(f32[8]{0:T(128)S(1)} %get-tuple-element.57, f32[8]{0:T(128)S(1)} %get-tuple-element.8), channel_id=1, replica_groups=mesh['sample'=2,'gz'=4,'gy'=4] {'gy'}, use_global_device_ids=true, to_apply=%region_1.2 | all-reduce | flops 16 | bytes 128 | tf_op jit(solution)/shard_map/psum | solution.py:64
  58.9 5.6 %all-reduce.4 = (f32[8]{0:T(128)S(1)}, f32[8]{0:T(128)S(1)}) all-reduce(f32[8]{0:T(128)S(1)} %get-tuple-element.2, f32[8]{0:T(128)S(1)} %get-tuple-element.3), channel_id=1, replica_groups=mesh['sample'=2,'gz'=4,'gy'=4] {'gz'}, use_global_device_ids=true, to_apply=%region_2.3 | all-reduce | flops 16 | bytes 128 | tf_op jit(solution)/shard_map/psum | solution.py:65
  64.6 1.2 convolution_bitcast_fusion
  65.8 1.0 copy-done.2
  66.7 0.3 fusion.40
  67.1 8.8 %psum.60 = f32[8]{0:T(128)S(1)} all-reduce(f32[8]{0:T(128)S(1)} %fusion.40), channel_id=1, replica_groups=mesh['sample'=2,'gz'=4,'gy'=4] {'gy'}, use_global_device_ids=true, to_apply=%region_9.10 | all-reduce | flops 8 | bytes 64 | tf_op jit(solution)/shard_map/psum | solution.py:64
  75.8 5.6 %psum.61 = f32[8]{0:T(128)S(1)} all-reduce(f32[8]{0:T(128)S(1)} %psum.60), channel_id=1, replica_groups=mesh['sample'=2,'gz'=4,'gy'=4] {'gz'}, use_global_device_ids=true, to_apply=%region_10.11 | all-reduce | flops 8 | bytes 64 | tf_op jit(solution)/shard_map/psum | solution.py:65
  81.5 1.5 %bitcast_add_fusion = f32[8,8,16,256]{3,2,1,0:T(8,128)S(1)} fusion(f32[8,8,2,2,8,128]{5,4,3,2,1,0:T(8,128)} %copy-done.2, f32[8]{0:T(128)S(1)} %div.10, f32[8,8,16,2,128]{4,2,3,1,0:T(8,128)S(1)} %get-tuple-element.58), kind=kLoop, calls=%fused_computation.59 | loop fusion | flops 524288 | bytes 3145760 | tf_op jit(solution)/shard_map/add | solution.py:104
  83.1 1.9 %collective-permute-start.8 = (f32[8,1,16,256]{3,2,1,0:T(8,128)S(1)}, f32[8,1,16,256]{3,2,1,0:T(8,128)S(1)}, u32[]{:S(2)}, u32[]{:S(2)}) collective-permute-start(f32[8,1,16,256]{3,2,1,0:T(8,128)S(1)} %get-tuple-element.16), channel_id=1, source_target_pairs={{0,4},{4,8},{8,12},{1,5},{5,9},{9,13},{2,6},{6,10},{10,14},{3,7},{... | collective-permute-start | bytes 393224 | tf_op jit(solution)/shard_map/ppermute | solution.py:25
  85.0 1.3 collective-permute-start.9
  86.3 3.4 %collective-permute-done.9 = f32[8,1,16,256]{3,2,1,0:T(8,128)S(1)} collective-permute-done((f32[8,1,16,256]{3,2,1,0:T(8,128)S(1)}, f32[8,1,16,256]{3,2,1,0:T(8,128)S(1)}, u32[]{:S(2)}, u32[]{:S(2)}) %collective-permute-start.9) | collective-permute-done | bytes 131104 | tf_op jit(solution)/shard_map/ppermute | solution.py:28
  89.7 0.1 pad_maximum_fusion.12
  89.8 3.5 %collective-permute-start.10 = (f32[8,10,1,256]{3,2,1,0:T(1,128)S(1)}, f32[8,10,1,256]{3,2,1,0:T(1,128)S(1)}, u32[]{:S(2)}, u32[]{:S(2)}) collective-permute-start(f32[8,10,1,256]{3,2,1,0:T(1,128)S(1)} %get-tuple-element.12), channel_id=1, source_target_pairs={{0,1},{1,2},{2,3},{4,5},{5,6},{6,7},{8,9},{9,10},{10,11},{12,13},{... | collective-permute-start | bytes 245768 | tf_op jit(solution)/shard_map/ppermute | solution.py:25
  93.3 1.5 %collective-permute-start.11 = (f32[8,10,1,256]{3,2,1,0:T(1,128)S(1)}, f32[8,10,1,256]{3,2,1,0:T(1,128)S(1)}, u32[]{:S(2)}, u32[]{:S(2)}) collective-permute-start(f32[8,10,1,256]{3,2,1,0:T(1,128)S(1)} %get-tuple-element.13), channel_id=1, source_target_pairs={{1,0},{2,1},{3,2},{5,4},{6,5},{7,6},{9,8},{10,9},{11,10},{13,12},{... | collective-permute-start | bytes 245768 | tf_op jit(solution)/shard_map/ppermute | solution.py:28
  94.8 0.6 collective-permute-done.10
  95.3 4.3 %collective-permute-done.11 = f32[8,10,1,256]{3,2,1,0:T(1,128)S(1)} collective-permute-done((f32[8,10,1,256]{3,2,1,0:T(1,128)S(1)}, f32[8,10,1,256]{3,2,1,0:T(1,128)S(1)}, u32[]{:S(2)}, u32[]{:S(2)}) %collective-permute-start.11) | collective-permute-done | bytes 81952 | tf_op jit(solution)/shard_map/ppermute | solution.py:28
  99.6 1.5 %select_maximum_fusion = f32[8,10,18,258]{3,2,1,0:T(8,128)S(1)} fusion(f32[8,10,1,256]{3,2,1,0:T(1,128)S(1)} %collective-permute-done.11, f32[8,10,1,256]{3,2,1,0:T(1,128)S(1)} %collective-permute-done.10, f32[8,1,16,256]{3,2,1,0:T(8,128)S(1)} %collective-permute-done.9, f32[8,8,16,256]{3,2,1,0:T(8,128)S(1)} %bitcast_add_fusion, ...), kind=kLoop, calls=%fused_computation.2 | loop fusion | flops 4458240 | bytes 2960640 | tf_op jit(solution)/shard_map/concatenate | solution.py:29
  101.1 2.4 %maximum_maximum_fusion = (f32[8,10,17,256]{3,2,1,0:T(8,128)}, f32[8,10,17,256]{3,2,1,0:T(8,128)}) fusion(f32[8,1,16,256]{3,2,1,0:T(8,128)S(1)} %collective-permute-done.9, f32[8,8,16,256]{3,2,1,0:T(8,128)S(1)} %bitcast_add_fusion, f32[8,1,16,256]{3,2,1,0:T(8,128)S(1)} %collective-permute-done.8, f32[8,10,1,256]{3,2,1,0:T(1,128)S(1)} %collective-permute-done.10, ...), kind=kLoop, calls=%fused_computation.17 | loop fusion | flops 2088960 | bytes 4259840 | tf_op jit(solution)/shard_map/concatenate | solution.py:29
  103.5 9.4 %multiply_reduce_fusion = (f32[8]{0:T(128)S(1)}, f32[8,8,16,256]{3,2,1,0:T(8,128)}) fusion(f32[8,8,16,256]{3,2,1,0:T(8,128)S(1)} %bitcast_add_fusion, f32[8,10,18,258]{3,2,1,0:T(8,128)S(1)} %select_maximum_fusion, f32[8,16,256]{2,1,0:T(8,128)} %get-tuple-element.37, f32[8,10,17,256]{3,2,1,0:T(8,128)} %get-tuple-element.11, ...), kind=kLoop, calls=%fused_computation.196 | loop fusion | flops 22020088 | bytes 30933060 | tf_op jit(solution)/shard_map/reduce_sum | solution.py:98
  112.9 8.4 %psum.62 = f32[8]{0:T(128)S(1)} all-reduce(f32[8]{0:T(128)S(1)} %get-tuple-element.6), channel_id=1, replica_groups=mesh['sample'=2,'gz'=4,'gy'=4] {'gy'}, use_global_device_ids=true, to_apply=%region_12.13 | all-reduce | flops 8 | bytes 64 | tf_op jit(solution)/shard_map/psum | solution.py:64
  121.3 6.8 %psum.63 = f32[8]{0:T(128)S(1)} all-reduce(f32[8]{0:T(128)S(1)} %psum.62), channel_id=1, replica_groups=mesh['sample'=2,'gz'=4,'gy'=4] {'gz'}, use_global_device_ids=true, to_apply=%region_13.14 | all-reduce | flops 8 | bytes 64 | tf_op jit(solution)/shard_map/psum | solution.py:65
  128.1 3.4 %multiply_subtract_fusion = (f32[8,8,16,256]{3,2,1,0:T(8,128)}, f32[8,8,16,256]{3,2,1,0:T(8,128)}) fusion(f32[8,8,16,256]{3,2,1,0:T(8,128)} %get-tuple-element.7, f32[8,8,16,256]{3,2,1,0:T(8,128)} %copy-done.1, f32[8]{0:T(128)S(1)} %div.11, f32[8,16,256]{2,1,0:T(8,128)S(1)} %copy-done.5, f32[8]{0:T(128)S(1)} %div.9, ...), kind=kLoop, calls=%fused_computation.194 | loop fusion | flops 1835008 | bytes 6422592 | tf_op jit(solution)/shard_map/sub | solution.py:101
  (45 shorter events, 0.4 us)
Async XLA Ops:
  0.6 6.2 %copy-start = (f32[8,128,128]{2,1,0:T(8,128)S(1)}, f32[8,128,128]{2,1,0:T(8,128)}, u32[]{:S(2)}) copy-start(f32[8,128,128]{2,1,0:T(8,128)} %param.13) | copy-start | bytes 1572868
  0.6 14.8 %copy-start.11 = (f32[16]{0:T(128)S(1)}, f32[16]{0:T(128)}, u32[]{:S(2)}) copy-start(f32[16]{0:T(128)} %param.11) | copy-start | bytes 196
  0.7 14.8 %copy-start.12 = (s32[8]{0:T(128)S(1)}, s32[8]{0:T(128)}, u32[]{:S(2)}) copy-start(s32[8]{0:T(128)} %param.10) | copy-start | bytes 100
  1.6 14.8 %collective-permute-start.1 = (f32[1,16,256]{1,2,0:T(8,128)S(1)}, f32[1,16,256]{1,2,0:T(8,128)S(1)}, u32[]{:S(2)}, u32[]{:S(2)}) collective-permute-start(f32[1,16,256]{1,2,0:T(8,128)S(1)} %get-tuple-element.54), channel_id=1, source_target_pairs={{4,0},{8,4},{12,8},{5,1},{9,5},{13,9},{6,2},{10,6},{14,10},{7,3},{... | collective-permute-start | bytes 49160 | tf_op jit(solution)/shard_map/ppermute | solution.py:28
  2.9 13.6 %collective-permute-start = (f32[1,16,256]{1,2,0:T(8,128)S(1)}, f32[1,16,256]{1,2,0:T(8,128)S(1)}, u32[]{:S(2)}, u32[]{:S(2)}) collective-permute-start(f32[1,16,256]{1,2,0:T(8,128)S(1)} %get-tuple-element.54), channel_id=1, source_target_pairs={{0,4},{4,8},{8,12},{1,5},{5,9},{9,13},{2,6},{6,10},{10,14},{3,7},{... | collective-permute-start | bytes 49160 | tf_op jit(solution)/shard_map/ppermute | solution.py:25
  8.0 1.0 copy-start.4
  9.0 18.5 %collective-permute-start.5 = (f32[8,1,16,256]{3,2,1,0:T(8,128)S(1)}, f32[8,1,16,256]{3,2,1,0:T(8,128)S(1)}, u32[]{:S(2)}, u32[]{:S(2)}) collective-permute-start(f32[8,1,16,256]{3,2,1,0:T(8,128)S(1)} %get-tuple-element.18), channel_id=1, source_target_pairs={{4,0},{8,4},{12,8},{5,1},{9,5},{13,9},{6,2},{10,6},{14,10},{7,3},{... | collective-permute-start | bytes 393224 | tf_op jit(solution)/shard_map/ppermute | solution.py:28
  10.3 17.1 %collective-permute-start.4 = (f32[8,1,16,256]{3,2,1,0:T(8,128)S(1)}, f32[8,1,16,256]{3,2,1,0:T(8,128)S(1)}, u32[]{:S(2)}, u32[]{:S(2)}) collective-permute-start(f32[8,1,16,256]{3,2,1,0:T(8,128)S(1)} %get-tuple-element.19), channel_id=1, source_target_pairs={{0,4},{4,8},{8,12},{1,5},{5,9},{9,13},{2,6},{6,10},{10,14},{3,7},{... | collective-permute-start | bytes 393224 | tf_op jit(solution)/shard_map/ppermute | solution.py:25
  16.6 5.5 %collective-permute-start.2 = (f32[10,1,256]{2,1,0:T(1,128)S(1)}, f32[10,1,256]{2,1,0:T(1,128)S(1)}, u32[]{:S(2)}, u32[]{:S(2)}) collective-permute-start(f32[10,1,256]{2,1,0:T(1,128)S(1)} %get-tuple-element.46), channel_id=1, source_target_pairs={{0,1},{1,2},{2,3},{4,5},{5,6},{6,7},{8,9},{9,10},{10,11},{12,13},{... | collective-permute-start | bytes 30728 | tf_op jit(solution)/shard_map/ppermute | solution.py:25
  20.1 5.6 %collective-permute-start.3 = (f32[10,1,256]{2,1,0:T(1,128)S(1)}, f32[10,1,256]{2,1,0:T(1,128)S(1)}, u32[]{:S(2)}, u32[]{:S(2)}) collective-permute-start(f32[10,1,256]{2,1,0:T(1,128)S(1)} %get-tuple-element.47), channel_id=1, source_target_pairs={{1,0},{2,1},{3,2},{5,4},{6,5},{7,6},{9,8},{10,9},{11,10},{13,12},{... | collective-permute-start | bytes 30728 | tf_op jit(solution)/shard_map/ppermute | solution.py:28
  27.4 11.7 %copy-start.6 = (f32[8,16,256]{2,1,0:T(8,128)}, f32[8,16,256]{2,1,0:T(8,128)S(1)}, u32[]{:S(2)}) copy-start(f32[8,16,256]{2,1,0:T(8,128)S(1)} %get-tuple-element.25) | copy-start | bytes 393220
  27.4 11.7 %copy-start.7 = (f32[8,16,256]{2,1,0:T(8,128)}, f32[8,16,256]{2,1,0:T(8,128)S(1)}, u32[]{:S(2)}) copy-start(f32[8,16,256]{2,1,0:T(8,128)S(1)} %get-tuple-element.26) | copy-start | bytes 393220
  27.4 11.6 %copy-start.9 = (f32[8,1,16,256]{3,2,1,0:T(8,128)}, f32[8,1,16,256]{3,2,1,0:T(8,128)S(1)}, u32[]{:S(2)}) copy-start(f32[8,1,16,256]{3,2,1,0:T(8,128)S(1)} %collective-permute-done.4) | copy-start | bytes 393220
  27.6 11.5 %copy-start.8 = (f32[8,1,16,256]{3,2,1,0:T(8,128)}, f32[8,1,16,256]{3,2,1,0:T(8,128)S(1)}, u32[]{:S(2)}) copy-start(f32[8,1,16,256]{3,2,1,0:T(8,128)S(1)} %collective-permute-done.5) | copy-start | bytes 393220
  27.6 11.5 %copy-start.3 = (f32[8,10,16,256]{3,2,1,0:T(8,128)}, f32[8,10,16,256]{3,2,1,0:T(8,128)S(1)}, u32[]{:S(2)}) copy-start(f32[8,10,16,256]{3,2,1,0:T(8,128)S(1)} %constant_dynamic-update-slice_fusion) | copy-start | bytes 3932164
  27.7 5.7 %collective-permute-start.6 = (f32[8,10,1,256]{3,2,1,0:T(1,128)S(1)}, f32[8,10,1,256]{3,2,1,0:T(1,128)S(1)}, u32[]{:S(2)}, u32[]{:S(2)}) collective-permute-start(f32[8,10,1,256]{3,2,1,0:T(1,128)S(1)} %get-tuple-element.14), channel_id=1, source_target_pairs={{0,1},{1,2},{2,3},{4,5},{5,6},{6,7},{8,9},{9,10},{10,11},{12,13},{... | collective-permute-start | bytes 245768 | tf_op jit(solution)/shard_map/ppermute | solution.py:25
  31.2 6.3 %collective-permute-start.7 = (f32[8,10,1,256]{3,2,1,0:T(1,128)S(1)}, f32[8,10,1,256]{3,2,1,0:T(1,128)S(1)}, u32[]{:S(2)}, u32[]{:S(2)}) collective-permute-start(f32[8,10,1,256]{3,2,1,0:T(1,128)S(1)} %get-tuple-element.15), channel_id=1, source_target_pairs={{1,0},{2,1},{3,2},{5,4},{6,5},{7,6},{9,8},{10,9},{11,10},{13,12},{... | collective-permute-start | bytes 245768 | tf_op jit(solution)/shard_map/ppermute | solution.py:28
  37.6 1.5 %copy-start.10 = (f32[8,10,1,256]{3,2,1,0:T(1,128)}, f32[8,10,1,256]{3,2,1,0:T(1,128)S(1)}, u32[]{:S(2)}) copy-start(f32[8,10,1,256]{3,2,1,0:T(1,128)S(1)} %collective-permute-done.7) | copy-start | bytes 245764
  39.1 25.4 %copy-start.5 = (f32[8,16,256]{2,1,0:T(8,128)S(1)}, f32[8,16,256]{2,1,0:T(8,128)}, u32[]{:S(2)}) copy-start(f32[8,16,256]{2,1,0:T(8,128)} %param.7) | copy-start | bytes 393220
  49.0 32.5 %copy-start.1 = (f32[8,8,16,256]{3,2,1,0:T(8,128)}, f32[8,8,16,256]{3,2,1,0:T(8,128)S(1)}, u32[]{:S(2)}) copy-start(f32[8,8,16,256]{3,2,1,0:T(8,128)S(1)} %get-tuple-element.9) | copy-start | bytes 3145732
  65.8 1.0 copy-start.2
  83.1 3.2 %collective-permute-start.8 = (f32[8,1,16,256]{3,2,1,0:T(8,128)S(1)}, f32[8,1,16,256]{3,2,1,0:T(8,128)S(1)}, u32[]{:S(2)}, u32[]{:S(2)}) collective-permute-start(f32[8,1,16,256]{3,2,1,0:T(8,128)S(1)} %get-tuple-element.16), channel_id=1, source_target_pairs={{0,4},{4,8},{8,12},{1,5},{5,9},{9,13},{2,6},{6,10},{10,14},{3,7},{... | collective-permute-start | bytes 393224 | tf_op jit(solution)/shard_map/ppermute | solution.py:25
  85.0 4.7 %collective-permute-start.9 = (f32[8,1,16,256]{3,2,1,0:T(8,128)S(1)}, f32[8,1,16,256]{3,2,1,0:T(8,128)S(1)}, u32[]{:S(2)}, u32[]{:S(2)}) collective-permute-start(f32[8,1,16,256]{3,2,1,0:T(8,128)S(1)} %get-tuple-element.17), channel_id=1, source_target_pairs={{4,0},{8,4},{12,8},{5,1},{9,5},{13,9},{6,2},{10,6},{14,10},{7,3},{... | collective-permute-start | bytes 393224 | tf_op jit(solution)/shard_map/ppermute | solution.py:28
  89.8 5.5 %collective-permute-start.10 = (f32[8,10,1,256]{3,2,1,0:T(1,128)S(1)}, f32[8,10,1,256]{3,2,1,0:T(1,128)S(1)}, u32[]{:S(2)}, u32[]{:S(2)}) collective-permute-start(f32[8,10,1,256]{3,2,1,0:T(1,128)S(1)} %get-tuple-element.12), channel_id=1, source_target_pairs={{0,1},{1,2},{2,3},{4,5},{5,6},{6,7},{8,9},{9,10},{10,11},{12,13},{... | collective-permute-start | bytes 245768 | tf_op jit(solution)/shard_map/ppermute | solution.py:25
  93.3 6.3 %collective-permute-start.11 = (f32[8,10,1,256]{3,2,1,0:T(1,128)S(1)}, f32[8,10,1,256]{3,2,1,0:T(1,128)S(1)}, u32[]{:S(2)}, u32[]{:S(2)}) collective-permute-start(f32[8,10,1,256]{3,2,1,0:T(1,128)S(1)} %get-tuple-element.13), channel_id=1, source_target_pairs={{1,0},{2,1},{3,2},{5,4},{6,5},{7,6},{9,8},{10,9},{11,10},{13,12},{... | collective-permute-start | bytes 245768 | tf_op jit(solution)/shard_map/ppermute | solution.py:28
where the time goes:
time: 132 us
  blocking collectives  45.2 us (34%)
  other arithmetic  34.4 us (26%)
  starting transfers between devices  28.4 us (22%)
  waiting for transfers between devices  15.9 us (12%)
  local copies, waits for them, and re-layouts  3.56 us (3%)
  matrix products  2.26 us (2%)
  between operations  1.71 us (1%)
    psum x3, blocking collectives, global_sum(): row_sum = lax.psum(values, 'gy')  27.1 us
    ppermute x6, starting transfers between devices, padded_2(): lax.ppermute(lax.slice_in_dim(block, block.shape[dim] - width, None, axis...  20.5 us
    reduce_sum x2, other arithmetic, on_device(): curvature = global_sum(jnp.sum(direction * image, axis=(1, 2, 3)))  19.2 us
    psum x3, blocking collectives, global_sum(): return lax.psum(row_sum, 'gz')  18.1 us
    ppermute x6, waiting for transfers between devices, padded_2(): lax.ppermute(lax.slice_in_dim(block, 0, width, axis=dim), axis, backward)  15.4 us
    ppermute x6, starting transfers between devices, padded_2(): lax.ppermute(lax.slice_in_dim(block, 0, width, axis=dim), axis, backward)  7.93 us
    concatenate x5, other arithmetic, padded_2(): block = jnp.concatenate([low, block, high], axis=dim)  5.62 us
    sub x1, other arithmetic, on_device(): residual = residual - alpha * image  3.39 us
  transfers between devices with their start and end apart: 12, of which 5 were waited for; matrix products, arithmetic and copies ran while one was open for 5% of the time, Pallas kernels for 0%

commit v1 on v0

v1 whole, which is shorter than its diff:
```python
import functools

import jax
import jax.numpy as jnp
from jax import lax
from jax.experimental import pallas as pl
from jax.experimental.pallas import tpu as pltpu
from jax.sharding import PartitionSpec as P

MESH = pl.DeviceIdType.MESH
EDGE = 8
REACH = 2
DIRECTIONS = [(dz, dy) for dz in (-1, 0, 1) for dy in (-1, 0, 1) if (dz, dy) != (0, 0)]


def slot(dz, dy):
    return (dz + 1) * 3 + dy + 1


def split(x):
    high = x.astype(jnp.bfloat16)
    low = (x - high.astype(jnp.float32)).astype(jnp.bfloat16)
    return high, low


def smooth_x(parts):
    width = parts[0].shape[1]
    lane = lax.broadcasted_iota(jnp.int32, parts[0].shape, 1)
    first, last = lane == 0, lane == width - 1
    rolled = [pltpu.roll(u, 1, 1) for u in parts]
    pairs = [
        u + jnp.where(first, rolled[i - 1] if i else 0.0, rolled[i]) for i, u in enumerate(parts)
    ]
    rolled = [pltpu.roll(h, width - 1, 1) for h in pairs]
    return [
        h + jnp.where(last, rolled[i + 1] if i + 1 < len(pairs) else parts[i], rolled[i])
        for i, h in enumerate(pairs)
    ]


def smooth_y(u):
    h = u + pltpu.roll(u, 1, 0)
    return h + pltpu.roll(h, u.shape[0] - 1, 0)


def smooth_xy(parts):
    return [smooth_y(u) for u in smooth_x(parts)]


def kernel(
    grid,
    right_ref,
    labels_ref,
    coeff_ref,
    index_ref,
    table_ref,
    step_ref,
    inverse_ref,
    solution_ref,
    residual_ref,
    r_ext,
    p_ext,
    q_ext,
    w_ext,
    y_own,
    weights,
    c_rows,
    label_rows,
    c_planes,
    diag,
    y_send,
    z_recv,
    y_recv,
    corner_recv,
    label_recv,
    message,
    gathered,
    coefs,
    out_s,
    out_r,
    send_sem,
    recv_sem,
    label_send_sem,
    label_recv_sem,
    gather_send_sem,
    gather_recv_sem,
    out_sem,
):
    n_gz, n_gy = grid
    group = n_gz * n_gy
    depth, rows, nx = right_ref.shape
    systems, lanes = inverse_ref.shape[0], inverse_ref.shape[1]
    halves = nx // lanes
    ring = r_ext.shape[2]
    y_blocks = labels_ref.shape[1]
    label_cols = labels_ref.shape[2]
    sample, gz, gy = lax.axis_index("sample"), lax.axis_index("gz"), lax.axis_index("gy")
    me = gz * n_gy + gy

    def has(dz, dy):
        z_ok = gz + dz >= 0 if dz < 0 else gz + dz < n_gz
        y_ok = gy + dy >= 0 if dy < 0 else gy + dy < n_gy
        return jnp.logical_and(z_ok, y_ok)

    def present(dz, dy):
        return jnp.where(has(dz, dy), 1.0, 0.0).astype(jnp.float32)

    def peer_of(offset):
        peer = lax.rem(me + offset, group)
        return peer, (sample, lax.div(peer, n_gy), lax.rem(peer, n_gy))

    z_recv[...] = jnp.zeros_like(z_recv)
    y_recv[...] = jnp.zeros_like(y_recv)
    corner_recv[...] = jnp.zeros_like(corner_recv)
    label_recv[...] = jnp.zeros_like(label_recv)
    y_send[0] = right_ref[:, 0:REACH, :]
    y_send[1] = right_ref[:, rows - REACH : rows, :]

    barrier = pltpu.get_barrier_semaphore()

    def greet(offset, carry):
        _, device = peer_of(offset)
        pl.semaphore_signal(barrier, inc=1, device_id=device, device_id_type=MESH)
        return carry

    lax.fori_loop(1, group, greet, 0)

    for m in range(systems):
        high, low = split(inverse_ref[m])
        weights[m, 0:lanes, 0:lanes] = high
        weights[m, lanes : 2 * lanes, 0:lanes] = high
        weights[m, 0:lanes, lanes : 2 * lanes] = low
        weights[m, lanes : 2 * lanes, lanes : 2 * lanes] = low
    r_ext[...] = jnp.zeros_like(r_ext)
    for h in range(halves):
        r_ext[h, REACH : REACH + depth, 0:rows, :] = right_ref[:, :, h * lanes : (h + 1) * lanes]

    pl.semaphore_wait(barrier, group - 1)

    def halo_copy(dz, dy):
        device = (sample, gz + dz, gy + dy)
        z_from = depth - REACH if dz > 0 else 0
        if dy == 0:
            source = right_ref.at[pl.ds(z_from, REACH)]
            target = z_recv.at[0 if dz > 0 else 1]
        elif dz == 0:
            source = y_send.at[1 if dy > 0 else 0]
            target = y_recv.at[0 if dy > 0 else 1]
        else:
            source = y_send.at[1 if dy > 0 else 0, pl.ds(z_from, REACH)]
            target = corner_recv.at[0 if dz > 0 else 1, 0 if dy > 0 else 1]
        return pltpu.make_async_remote_copy(
            src_ref=source,
            dst_ref=target,
            send_sem=send_sem.at[slot(dz, dy)],
            recv_sem=recv_sem.at[slot(-dz, -dy)],
            device_id=device,
            device_id_type=MESH,
        )

    def label_copy(dz, dy):
        return pltpu.make_async_remote_copy(
            src_ref=labels_ref,
            dst_ref=label_recv.at[slot(-dz, -dy)],
            send_sem=label_send_sem.at[slot(dz, dy)],
            recv_sem=label_recv_sem.at[slot(-dz, -dy)],
            device_id=(sample, gz + dz, gy + dy),
            device_id_type=MESH,
        )

    for dz, dy in DIRECTIONS:

        @pl.when(has(dz, dy))
        def _(dz=dz, dy=dy):
            label_copy(dz, dy).start()
            halo_copy(dz, dy).start()

    for dz, dy in DIRECTIONS:

        @pl.when(has(dz, dy))
        def _(dz=dz, dy=dy):
            label_copy(-dz, -dy).wait_recv()
            halo_copy(-dz, -dy).wait_recv()

    for h in range(halves):
        cut = slice(h * lanes, (h + 1) * lanes)
        for side in (0, 1):
            planes = slice(0, REACH) if side == 0 else slice(REACH + depth, 2 * REACH + depth)
            r_ext[h, planes, 0:rows, :] = z_recv[side, :, :, cut]
            r_ext[h, planes, rows : rows + REACH, :] = corner_recv[side, 1, :, :, cut]
            r_ext[h, planes, ring - REACH : ring, :] = corner_recv[side, 0, :, :, cut]
        own = slice(REACH, REACH + depth)
        r_ext[h, own, rows : rows + REACH, :] = y_recv[1, :, :, cut]
        r_ext[h, own, ring - REACH : ring, :] = y_recv[0, :, :, cut]

    label_rows[...] = jnp.zeros_like(label_rows)
    for s in range(9):
        table = labels_ref[0] if s == slot(0, 0) else label_recv[s, 0]
        label_rows[s * y_blocks : (s + 1) * y_blocks, :] = table.astype(jnp.float32)
    spread = jnp.where(
        lax.broadcasted_iota(jnp.int32, (label_cols, nx), 0)
        == lax.broadcasted_iota(jnp.int32, (label_cols, nx), 1) // EDGE,
        1.0,
        0.0,
    ).astype(jnp.bfloat16)
    wide = jnp.dot(
        label_rows[...].astype(jnp.bfloat16), spread, preferred_element_type=jnp.float32
    )
    cells = jnp.zeros_like(wide)
    scale = step_ref[0] * 0.125
    for region in range(coeff_ref.shape[0]):
        cells = jnp.where(wide == float(region), coeff_ref[region] * scale, cells)
    c_rows[...] = cells

    sub = lax.broadcasted_iota(jnp.int32, (EDGE, lanes), 0)
    for dz in (-1, 0, 1):
        for h in range(halves):
            cut = slice(h * lanes, (h + 1) * lanes)

            def row(dy, block):
                at = slot(dz, dy) * y_blocks + block
                value = c_rows[at : at + 1, cut]
                if (dz, dy) != (0, 0):
                    value = value * present(dz, dy)
                return jnp.broadcast_to(value, (EDGE, lanes))

            for block in range(y_blocks):
                c_planes[dz + 1, h, block * EDGE : (block + 1) * EDGE, :] = row(0, block)
            c_planes[dz + 1, h, rows:ring, :] = jnp.where(
                sub < EDGE // 2, row(1, 0), row(-1, y_blocks - 1)
            )

    smooth = [smooth_xy([c_planes[d, h] for h in range(halves)]) for d in range(3)]
    for h in range(halves):
        low, own, high = (smooth[d][h] for d in range(3))
        diag[0, h] = 3.0 * low + own + 64.0 * c_planes[0, h]
        diag[1, h] = low + 3.0 * own + 64.0 * c_planes[1, h]
        diag[2, h] = 4.0 * own + 64.0 * c_planes[1, h]
        diag[3, h] = high + 3.0 * own + 64.0 * c_planes[1, h]
        diag[4, h] = 3.0 * high + own + 64.0 * c_planes[2, h]

    ring_row = lax.broadcasted_iota(jnp.int32, (ring, lanes), 0)
    row_mask = jnp.where(
        ring_row < rows,
        1.0,
        jnp.where(ring_row < rows + EDGE // 2, present(0, 1), present(0, -1)),
    )

    def apply(field, z, shift):
        def c_of(plane):
            return 0 if plane < 0 else 2 if plane >= depth else 1

        below, here, above = field(z - 1), field(z), field(z + 1)
        kind = 0 if z < 0 else 4 if z >= depth else 1 if z == 0 else 3 if z == depth - 1 else 2
        ku, kcu = [], []
        for h in range(halves):
            u = (below[h] + here[h]) + (here[h] + above[h])
            if kind == 2:
                cu = c_planes[1, h] * u
            else:
                cu = (
                    c_planes[c_of(z - 1), h] * below[h]
                    + 2.0 * (c_planes[c_of(z), h] * here[h])
                    + c_planes[c_of(z + 1), h] * above[h]
                )
            ku.append(u)
            kcu.append(cu)
        ku, kcu = smooth_xy(ku), smooth_xy(kcu)
        return [
            (diag[kind, h] + shift) * here[h] - c_planes[c_of(z), h] * ku[h] - kcu[h]
            for h in range(halves)
        ]

    def product(x, m):
        shape = x.shape
        flat = x.reshape(-1, lanes)
        high, low = split(flat)
        both = jnp.dot(
            jnp.concatenate([high, low], axis=1), weights[m], preferred_element_type=jnp.float32
        )
        return (both[:, 0:lanes] + both[:, lanes : 2 * lanes]).reshape(shape)

    def fold(total, term):
        term = term.reshape(-1, 8, lanes)
        for i in range(term.shape[0]):
            total = total + term[i]
        return total

    def put(quantity, m, total):
        value = jnp.sum(jnp.sum(total, axis=0, keepdims=True), axis=1, keepdims=True)
        coefs[quantity, pl.ds(m, 1), :] = jnp.broadcast_to(value, (1, lanes))

    zero = jnp.zeros((8, lanes), jnp.float32)

    def first(m, carry):
        shift = table_ref[index_ref[m]]
        p_ext[m] = product(r_ext[...], m)
        a, c = zero, zero
        for z in range(-1, depth + 1):
            image = apply(
                lambda k: [p_ext[m, h, k + REACH] for h in range(halves)], z, shift
            )
            for h in range(halves):
                value = image[h] * row_mask
                if z < 0:
                    value = value * present(-1, 0)
                elif z >= depth:
                    value = value * present(1, 0)
                else:
                    p = p_ext[m, h, z + REACH, 0:rows, :]
                    a = fold(a, p * r_ext[h, z + REACH, 0:rows, :])
                    c = fold(c, p * value[0:rows])
                q_ext[m, h, z + 1] = value
        put(0, m, a)
        put(1, m, c)
        return carry

    lax.fori_loop(0, systems, first, 0)

    a_own, c_own = coefs[0], coefs[1]
    sigma = jnp.where(a_own > 0.0, c_own / jnp.where(a_own > 0.0, a_own, 1.0), 0.0)
    coefs[5] = sigma

    def second(m, carry):
        shift = table_ref[index_ref[m]]
        s_row = coefs[5, pl.ds(m, 1), :]
        q_shifted = q_ext[m] - s_row[None, None] * r_ext[:, 1 : REACH + depth + 1]
        w_ext[m] = product(q_shifted, m)
        g, f, e = zero, zero, zero
        for z in range(depth):
            image = apply(lambda k: [w_ext[m, h, k + 1] for h in range(halves)], z, shift)
            for h in range(halves):
                y = image[h][0:rows]
                w = w_ext[m, h, z + 1, 0:rows, :]
                q = q_ext[m, h, z + 1, 0:rows, :] - s_row * r_ext[h, z + REACH, 0:rows, :]
                g = fold(g, w * q)
                f = fold(f, p_ext[m, h, z + REACH, 0:rows, :] * y)
                e = fold(e, w * y)
                y_own[m, h, z] = y
        put(2, m, g)
        put(3, m, f)
        put(4, m, e)
        return carry

    lax.fori_loop(0, systems, second, 0)

    lane = lax.broadcasted_iota(jnp.int32, (systems, lanes), 1)
    packed = coefs[0]
    for quantity in range(1, 6):
        packed = jnp.where(lane == quantity, coefs[quantity], packed)
    message[...] = packed
    gathered[me] = packed

    def gather_copy(device, source):
        return pltpu.make_async_remote_copy(
            src_ref=message,
            dst_ref=gathered.at[source],
            send_sem=gather_send_sem.at[source],
            recv_sem=gather_recv_sem.at[source],
            device_id=device,
            device_id_type=MESH,
        )

    def send_to(offset):
        peer, device = peer_of(offset)
        return pltpu.make_async_remote_copy(
            src_ref=message,
            dst_ref=gathered.at[me],
            send_sem=gather_send_sem.at[peer],
            recv_sem=gather_recv_sem.at[me],
            device_id=device,
            device_id_type=MESH,
        )

    def send_step(offset, carry):
        send_to(offset).start()
        return carry

    lax.fori_loop(1, group, send_step, 0)

    def receive_step(offset, carry):
        peer, device = peer_of(offset)
        gather_copy(device, peer).wait_recv()
        return carry

    lax.fori_loop(1, group, receive_step, 0)

    def column(source, quantity):
        return jnp.broadcast_to(
            gathered[source][:, quantity : quantity + 1], (systems, lanes)
        )

    a_all = [column(d, 0) for d in range(group)]
    c_all = [column(d, 1) for d in range(group)]
    rz_0, curvature_0 = sum(a_all), sum(c_all)
    alpha_0 = rz_0 / curvature_0
    kept = [1.0 - alpha_0 * column(d, 5) for d in range(group)]
    g_all = [column(d, 2) for d in range(group)]
    rz_1 = sum(
        kept[d] * kept[d] * a_all[d] + alpha_0 * alpha_0 * g_all[d] for d in range(group)
    )
    beta = rz_1 / rz_0
    curvature_1 = zero
    for d in range(group):
        k = kept[d] + beta
        curvature_1 = curvature_1 + (
            k * k * c_all[d]
            - alpha_0 * k * (column(d, 3) + g_all[d])
            + alpha_0 * alpha_0 * column(d, 4)
        )
    alpha_1 = rz_1 / curvature_1
    own_k = 1.0 - alpha_0 * sigma + beta
    coefs[0] = alpha_0 + alpha_1 * own_k
    coefs[1] = alpha_0 * alpha_1

    def out_copies(m):
        return (
            pltpu.make_async_copy(out_s.at[m], solution_ref.at[m], out_sem.at[0, m]),
            pltpu.make_async_copy(out_r.at[m], residual_ref.at[m], out_sem.at[1, m]),
        )

    def finish(m, carry):
        main = coefs[0, pl.ds(m, 1), :][None]
        side = coefs[1, pl.ds(m, 1), :][None]
        own = slice(REACH, REACH + depth)
        for h in range(halves):
            cut = slice(h * lanes, (h + 1) * lanes)
            out_s[m, :, :, cut] = (
                main * p_ext[m, h, own, 0:rows, :] - side * w_ext[m, h, 1 : depth + 1, 0:rows, :]
            )
            out_r[m, :, :, cut] = (
                right_ref[:, :, cut]
                - main * q_ext[m, h, 1 : depth + 1, 0:rows, :]
                + side * y_own[m, h]
            )
        for copy in out_copies(m):
            copy.start()
        return carry

    lax.fori_loop(0, systems, finish, 0)

    def close_out(m, carry):
        for copy in out_copies(m):
            copy.wait()
        return carry

    lax.fori_loop(0, systems, close_out, 0)

    def close_send(offset, carry):
        send_to(offset).wait_send()
        return carry

    lax.fori_loop(1, group, close_send, 0)
    for dz, dy in DIRECTIONS:

        @pl.when(has(dz, dy))
        def _(dz=dz, dy=dy):
            label_copy(dz, dy).wait_send()
            halo_copy(dz, dy).wait_send()


def on_device(
    grid, right_side, labels, region_coeff, shift_index, shift_table, time_step, block_inverse
):
    depth, rows, nx = right_side.shape
    systems, lanes = block_inverse.shape[0], block_inverse.shape[1]
    halves = nx // lanes
    assert depth == EDGE and labels.shape[0] == 1
    group = grid[0] * grid[1]
    ring = rows + EDGE
    y_blocks = labels.shape[1]
    label_pad = -(-9 * y_blocks // 8) * 8
    f32 = jnp.float32
    vmem = pl.BlockSpec(memory_space=pltpu.VMEM)
    smem = pl.BlockSpec(memory_space=pltpu.SMEM)
    hbm = pl.BlockSpec(memory_space=pl.ANY)
    out = jax.ShapeDtypeStruct((systems,) + right_side.shape, f32)
    dma = pltpu.SemaphoreType.DMA
    return pl.pallas_call(
        functools.partial(kernel, grid),
        out_shape=(out, out),
        in_specs=[vmem, vmem, smem, smem, smem, smem, vmem],
        out_specs=(hbm, hbm),
        scratch_shapes=[
            pltpu.VMEM((halves, depth + 2 * REACH, ring, lanes), f32),
            pltpu.VMEM((systems, halves, depth + 2 * REACH, ring, lanes), f32),
            pltpu.VMEM((systems, halves, depth + 2, ring, lanes), f32),
            pltpu.VMEM((systems, halves, depth + 2, ring, lanes), f32),
            pltpu.VMEM((systems, halves, depth, rows, lanes), f32),
            pltpu.VMEM((systems, 2 * lanes, 2 * lanes), jnp.bfloat16),
            pltpu.VMEM((label_pad, nx), f32),
            pltpu.VMEM((label_pad, labels.shape[2]), f32),
            pltpu.VMEM((3, halves, ring, lanes), f32),
            pltpu.VMEM((5, halves, ring, lanes), f32),
            pltpu.VMEM((2, depth, REACH, nx), f32),
            pltpu.VMEM((2, REACH, rows, nx), f32),
            pltpu.VMEM((2, depth, REACH, nx), f32),
            pltpu.VMEM((2, 2, REACH, REACH, nx), f32),
            pltpu.VMEM((9,) + labels.shape, jnp.int32),
            pltpu.VMEM((systems, lanes), f32),
            pltpu.VMEM((group, systems, lanes), f32),
            pltpu.VMEM((6, systems, lanes), f32),
            pltpu.VMEM(out.shape, f32),
            pltpu.VMEM(out.shape, f32),
            dma((9,)),
            dma((9,)),
            dma((9,)),
            dma((9,)),
            dma((group,)),
            dma((group,)),
            dma((2, systems)),
        ],
        compiler_params=pltpu.CompilerParams(
            collective_id=0, has_side_effects=True, vmem_limit_bytes=40 * 1024 * 1024
        ),
    )(right_side, labels, region_coeff, shift_index, shift_table, time_step, block_inverse)


def solution(mesh):
    in_specs = (
        P(("sample", "gz"), "gy", None),
        P(("sample", "gz"), "gy", None),
        P("sample"),
        P("sample"),
        P(),
        P("sample"),
        P(),
    )
    out_specs = (P(None, ("sample", "gz"), "gy", None), P(None, ("sample", "gz"), "gy", None))
    grid = (mesh.shape["gz"], mesh.shape["gy"])
    return jax.shard_map(
        functools.partial(on_device, grid),
        mesh=mesh,
        in_specs=in_specs,
        out_specs=out_specs,
        check_vma=False,
    )
```

time: 132 us -> 34 us (0.26)
  blocking collectives: 45.2 us -> 0 us
  other arithmetic: 34.4 us -> 0 us
  starting transfers between devices: 28.4 us -> 0 us
  Pallas kernels: 0 us -> 27.2 us
  waiting for transfers between devices: 15.9 us -> 0 us
  matrix products: 2.26 us -> 0 us
  local copies, waits for them, and re-layouts: 3.56 us -> 5.2 us
    psum x6 -> x0, blocking collectives: 45.2 us -> none  [the longest x3 27.1 us: global_sum(): row_sum = lax.psum(values, 'gy')]
    ppermute x12 -> x0, starting transfers between devices: 28.4 us -> none  [the longest x6 20.5 us: padded_2(): lax.ppermute(lax.slice_in_dim(block, block.shape[dim] - width, None, axis...]
    pallas_call x0 -> x1, Pallas kernels: none -> 27.2 us  [on_device(): pl.pallas_call(functools.partial(kernel, grid), out_shape=(out, out), in_...]
    reduce_sum x5 -> x0, other arithmetic: 20.6 us -> none  [the longest x2 19.2 us: on_device(): curvature = global_sum(jnp.sum(direction * image, axis=(1, 2, 3)))]
    ppermute x12 -> x0, waiting for transfers between devices: 15.9 us -> none  [the longest x6 15.4 us: padded_2(): lax.ppermute(lax.slice_in_dim(block, 0, width, axis=dim), axis, backward)]
    concatenate x5 -> x0, other arithmetic: 5.62 us -> none  [padded_2(): block = jnp.concatenate([low, block, high], axis=dim)]
    sub x1 -> x0, other arithmetic: 3.39 us -> none  [on_device(): residual = residual - alpha * image]
    mul x3 -> x0, other arithmetic: 3.16 us -> none  [stencil(): weight * 0.5 * (conductivity + cond_beside) * (field - beside)]
  transfers between devices with their start and end apart: 12 -> 0, of which waited for: 5 -> 0; matrix products, arithmetic and copies ran while one was open for 5% -> 0% of each run, Pallas kernels for 0% -> 0%
where the time goes in v1:
time: 34 us; the launch traced here: 33.8 us
  Pallas kernels  27.2 us (80%)
  local copies, waits for them, and re-layouts  5.2 us (15%)
  between operations  1.35 us (4%)
    pallas_call x1, Pallas kernels, on_device(): pl.pallas_call(functools.partial(kernel, grid), out_shape=(out, out), in_...  27.2 us
    unnamed x14, local copies, waits for them, and re-layouts  5.2 us

profile of v1, /device:TPU:0, one launch (start us, length us, event | category | flops | bytes accessed | tf_op | source)
XLA Modules:
  0.0 33.8 jit_solution(7487457252804256642)
XLA Ops:
  0.6 0.0 copy-start.3
  0.6 0.0 copy-start.2
  1.3 0.0 copy-done.3
  1.3 0.0 copy-done.2
  1.3 0.0 copy-start
  1.3 1.0 %copy-done = f32[8,128,128]{2,1,0:T(8,128)S(1)} copy-done((f32[8,128,128]{2,1,0:T(8,128)S(1)}, f32[8,128,128]{2,1,0:T(8,128)}, u32[]{:S(2)}) %copy-start) | copy-done | bytes 524312
  2.4 0.0 copy-start.1
  2.4 0.9 %copy-done.1 = f32[8,16,256]{2,1,0:T(8,128)S(1)} copy-done((f32[8,16,256]{2,1,0:T(8,128)S(1)}, f32[8,16,256]{2,1,0:T(8,128)}, u32[]{:S(2)}) %copy-start.1) | copy-done | bytes 131096
  3.3 0.0 copy-start.4
  3.3 0.7 %copy-done.4 = s32[8]{0:T(128)S(1)} copy-done((s32[8]{0:T(128)S(1)}, s32[8]{0:T(128)}, u32[]{:S(2)}) %copy-start.4) | copy-done | bytes 56
  3.9 0.0 copy-start.5
  3.9 0.7 %copy-done.5 = f32[16]{0:T(128)S(1)} copy-done((f32[16]{0:T(128)S(1)}, f32[16]{0:T(128)}, u32[]{:S(2)}) %copy-start.5) | copy-done | bytes 88
  4.6 27.2 %shard_map.86 = (f32[8,8,16,256]{3,2,1,0:T(8,128)S(1)}, f32[8,8,16,256]{3,2,1,0:T(8,128)S(1)}) custom-call(f32[8,16,256]{2,1,0:T(8,128)S(1)} %copy-done.1, s32[1,2,32]{2,1,0:T(2,128)S(1)} %copy-done.2, f32[8]{0:T(128)S(1)} %copy-done.3, s32[8]{0:T(128)S(1)} %copy-done.4, f32[16]{0:T(128)S(1)} %copy-done.5, f32[1]{0:T(128)S(6)} %copy.11.step_ref, ...), custom_call_target="tpu_custom_call" | custom-call | tf_op jit(solution)/shard_map/pallas_call | solution.py:479
  31.8 1.0 %copy.12 = f32[8,8,16,256]{3,2,1,0:T(8,128)} copy(f32[8,8,16,256]{3,2,1,0:T(8,128)S(1)} %get-tuple-element.4) | data formatting | bytes 2097152
  32.8 1.0 %copy.13 = f32[8,8,16,256]{3,2,1,0:T(8,128)} copy(f32[8,8,16,256]{3,2,1,0:T(8,128)S(1)} %get-tuple-element.5) | data formatting | bytes 2097152
Async XLA Ops:
  0.6 0.7 %copy-start.3 = (f32[8]{0:T(128)S(1)}, f32[8]{0:T(128)}, u32[]{:S(2)}) copy-start(f32[8]{0:T(128)} %coeff_ref.1) | copy-start | bytes 100
  0.6 0.7 %copy-start.2 = (s32[1,2,32]{2,1,0:T(2,128)S(1)}, s32[1,2,32]{2,1,0:T(2,128)}, u32[]{:S(2)}) copy-start(s32[1,2,32]{2,1,0:T(2,128)} %labels_ref.1) | copy-start | bytes 772
  1.3 1.0 %copy-start = (f32[8,128,128]{2,1,0:T(8,128)S(1)}, f32[8,128,128]{2,1,0:T(8,128)}, u32[]{:S(2)}) copy-start(f32[8,128,128]{2,1,0:T(8,128)} %inverse_ref.1) | copy-start | bytes 1572868
  2.4 0.9 %copy-start.1 = (f32[8,16,256]{2,1,0:T(8,128)S(1)}, f32[8,16,256]{2,1,0:T(8,128)}, u32[]{:S(2)}) copy-start(f32[8,16,256]{2,1,0:T(8,128)} %right_ref.1) | copy-start | bytes 393220
  3.3 0.7 %copy-start.4 = (s32[8]{0:T(128)S(1)}, s32[8]{0:T(128)}, u32[]{:S(2)}) copy-start(s32[8]{0:T(128)} %index_ref.1) | copy-start | bytes 100
  3.9 0.7 %copy-start.5 = (f32[16]{0:T(128)S(1)}, f32[16]{0:T(128)}, u32[]{:S(2)}) copy-start(f32[16]{0:T(128)} %table_ref.1) | copy-start | bytes 196

commit v2 on v1

--- a/solution.py
+++ b/solution.py
@@ -49,6 +49,19 @@
 
 def kernel(
     grid,
+    right_hbm,
+    labels_hbm,
+    coeff_hbm,
+    index_hbm,
+    table_hbm,
+    step_hbm,
+    inverse_hbm,
+    r_ext,
+    p_ext,
+    q_ext,
+    w_ext,
+    y_own,
+    coefs,
     right_ref,
     labels_ref,
     coeff_ref,
@@ -56,13 +69,6 @@
     table_ref,
     step_ref,
     inverse_ref,
-    solution_ref,
-    residual_ref,
-    r_ext,
-    p_ext,
-    q_ext,
-    w_ext,
-    y_own,
     weights,
     c_rows,
     label_rows,
@@ -75,16 +81,14 @@
     label_recv,
     message,
     gathered,
-    coefs,
-    out_s,
-    out_r,
+    load_sem,
+    near_sem,
     send_sem,
     recv_sem,
     label_send_sem,
     label_recv_sem,
     gather_send_sem,
     gather_recv_sem,
-    out_sem,
 ):
     n_gz, n_gy = grid
     group = n_gz * n_gy
@@ -109,33 +113,56 @@
         peer = lax.rem(me + offset, group)
         return peer, (sample, lax.div(peer, n_gy), lax.rem(peer, n_gy))
 
+    loads = [
+        pltpu.make_async_copy(source, target, load_sem.at[i])
+        for i, (source, target) in enumerate(
+            (
+                (right_hbm, right_ref),
+                (labels_hbm, labels_ref),
+                (inverse_hbm, inverse_ref),
+                (coeff_hbm, coeff_ref),
+                (step_hbm, step_ref),
+                (index_hbm, index_ref),
+                (table_hbm, table_ref),
+            )
+        )
+    ]
+    for load in loads:
+        load.start()
+
     z_recv[...] = jnp.zeros_like(z_recv)
     y_recv[...] = jnp.zeros_like(y_recv)
     corner_recv[...] = jnp.zeros_like(corner_recv)
     label_recv[...] = jnp.zeros_like(label_recv)
+
+    barrier = pltpu.get_barrier_semaphore()
+
+    def signal_near(semaphore):
+        for dz, dy in DIRECTIONS:
+
+            @pl.when(has(dz, dy))
+            def _(dz=dz, dy=dy):
+                pl.semaphore_signal(
+                    semaphore,
+                    inc=1,
+                    device_id=(sample, gz + dz, gy + dy),
+                    device_id_type=MESH,
+                )
+
+    z_near = 1 + (gz > 0).astype(jnp.int32) + (gz < n_gz - 1).astype(jnp.int32)
+    y_near = 1 + (gy > 0).astype(jnp.int32) + (gy < n_gy - 1).astype(jnp.int32)
+    near = z_near * y_near - 1
+
+    signal_near(barrier)
+    r_ext[...] = jnp.zeros_like(r_ext)
+    loads[0].wait()
+    loads[1].wait()
     y_send[0] = right_ref[:, 0:REACH, :]
     y_send[1] = right_ref[:, rows - REACH : rows, :]
-
-    barrier = pltpu.get_barrier_semaphore()
-
-    def greet(offset, carry):
-        _, device = peer_of(offset)
-        pl.semaphore_signal(barrier, inc=1, device_id=device, device_id_type=MESH)
-        return carry
-
-    lax.fori_loop(1, group, greet, 0)
-
-    for m in range(systems):
-        high, low = split(inverse_ref[m])
-        weights[m, 0:lanes, 0:lanes] = high
-        weights[m, lanes : 2 * lanes, 0:lanes] = high
-        weights[m, 0:lanes, lanes : 2 * lanes] = low
-        weights[m, lanes : 2 * lanes, lanes : 2 * lanes] = low
-    r_ext[...] = jnp.zeros_like(r_ext)
     for h in range(halves):
         r_ext[h, REACH : REACH + depth, 0:rows, :] = right_ref[:, :, h * lanes : (h + 1) * lanes]
 
-    pl.semaphore_wait(barrier, group - 1)
+    pl.semaphore_wait(barrier, near)
 
     def halo_copy(dz, dy):
         device = (sample, gz + dz, gy + dy)
@@ -175,12 +202,39 @@
             label_copy(dz, dy).start()
             halo_copy(dz, dy).start()
 
+    for load in loads[2:]:
+        load.wait()
+    for m in range(systems):
+        high, low = split(inverse_ref[m])
+        weights[m, 0:lanes, 0:lanes] = high
+        weights[m, lanes : 2 * lanes, 0:lanes] = high
+        weights[m, 0:lanes, lanes : 2 * lanes] = low
+        weights[m, lanes : 2 * lanes, lanes : 2 * lanes] = low
+
+    def pieces(x):
+        return jnp.concatenate(split(x.reshape(-1, lanes)), axis=1)
+
+    def product(x, m):
+        both = jnp.dot(x, weights[m], preferred_element_type=jnp.float32)
+        return both[:, 0:lanes] + both[:, lanes : 2 * lanes]
+
+    own_planes = slice(REACH, REACH + depth)
+    own_pieces = pieces(r_ext[:, own_planes, 0:rows, :])
+    for m in range(systems):
+        p_ext[m, :, own_planes, 0:rows, :] = product(own_pieces, m).reshape(
+            halves, depth, rows, lanes
+        )
+
     for dz, dy in DIRECTIONS:
 
         @pl.when(has(dz, dy))
         def _(dz=dz, dy=dy):
             label_copy(-dz, -dy).wait_recv()
             halo_copy(-dz, -dy).wait_recv()
+
+    rounds = max(n_gz, n_gy) - 3
+    if rounds > 0:
+        signal_near(near_sem.at[0])
 
     for h in range(halves):
         cut = slice(h * lanes, (h + 1) * lanes)
@@ -271,15 +325,6 @@
             for h in range(halves)
         ]
 
-    def product(x, m):
-        shape = x.shape
-        flat = x.reshape(-1, lanes)
-        high, low = split(flat)
-        both = jnp.dot(
-            jnp.concatenate([high, low], axis=1), weights[m], preferred_element_type=jnp.float32
-        )
-        return (both[:, 0:lanes] + both[:, lanes : 2 * lanes]).reshape(shape)
-
     def fold(total, term):
         term = term.reshape(-1, 8, lanes)
         for i in range(term.shape[0]):
@@ -292,9 +337,22 @@
 
     zero = jnp.zeros((8, lanes), jnp.float32)
 
+    z_pieces = [
+        pieces(r_ext[:, planes])
+        for planes in (slice(0, REACH), slice(REACH + depth, 2 * REACH + depth))
+    ]
+    y_pieces = pieces(r_ext[:, own_planes, rows:ring, :])
+    for m in range(systems):
+        for planes, x in zip(
+            (slice(0, REACH), slice(REACH + depth, 2 * REACH + depth)), z_pieces
+        ):
+            p_ext[m, :, planes] = product(x, m).reshape(halves, REACH, ring, lanes)
+        p_ext[m, :, own_planes, rows:ring, :] = product(y_pieces, m).reshape(
+            halves, depth, ring - rows, lanes
+        )
+
     def first(m, carry):
         shift = table_ref[index_ref[m]]
-        p_ext[m] = product(r_ext[...], m)
         a, c = zero, zero
         for z in range(-1, depth + 1):
             image = apply(
@@ -325,7 +383,7 @@
         shift = table_ref[index_ref[m]]
         s_row = coefs[5, pl.ds(m, 1), :]
         q_shifted = q_ext[m] - s_row[None, None] * r_ext[:, 1 : REACH + depth + 1]
-        w_ext[m] = product(q_shifted, m)
+        w_ext[m] = product(pieces(q_shifted), m).reshape(q_shifted.shape)
         g, f, e = zero, zero, zero
         for z in range(depth):
             image = apply(lambda k: [w_ext[m, h, k + 1] for h in range(halves)], z, shift)
@@ -343,6 +401,11 @@
         return carry
 
     lax.fori_loop(0, systems, second, 0)
+
+    for r in range(rounds):
+        pl.semaphore_wait(near_sem.at[r], near)
+        if r + 1 < rounds:
+            signal_near(near_sem.at[r + 1])
 
     lane = lax.broadcasted_iota(jnp.int32, (systems, lanes), 1)
     packed = coefs[0]
@@ -413,50 +476,43 @@
     coefs[0] = alpha_0 + alpha_1 * own_k
     coefs[1] = alpha_0 * alpha_1
 
-    def out_copies(m):
-        return (
-            pltpu.make_async_copy(out_s.at[m], solution_ref.at[m], out_sem.at[0, m]),
-            pltpu.make_async_copy(out_r.at[m], residual_ref.at[m], out_sem.at[1, m]),
-        )
-
-    def finish(m, carry):
-        main = coefs[0, pl.ds(m, 1), :][None]
-        side = coefs[1, pl.ds(m, 1), :][None]
-        own = slice(REACH, REACH + depth)
+    def close_send(offset, carry):
+        send_to(offset).wait_send()
+        return carry
+
+    lax.fori_loop(1, group, close_send, 0)
+    for dz, dy in DIRECTIONS:
+
+        @pl.when(has(dz, dy))
+        def _(dz=dz, dy=dy):
+            label_copy(dz, dy).wait_send()
+            halo_copy(dz, dy).wait_send()
+
+
+def finish(
+    r_ext, p_ext, q_ext, w_ext, y_own, coefs, solution_ref, residual_ref, out_s, out_r, out_sem
+):
+    systems, halves, depth, rows, lanes = y_own.shape
+    own = slice(REACH, REACH + depth)
+    copies = []
+    for m in range(systems):
+        main = coefs[0, m : m + 1, :][None]
+        side = coefs[1, m : m + 1, :][None]
         for h in range(halves):
             cut = slice(h * lanes, (h + 1) * lanes)
             out_s[m, :, :, cut] = (
                 main * p_ext[m, h, own, 0:rows, :] - side * w_ext[m, h, 1 : depth + 1, 0:rows, :]
             )
             out_r[m, :, :, cut] = (
-                right_ref[:, :, cut]
+                r_ext[h, own, 0:rows, :]
                 - main * q_ext[m, h, 1 : depth + 1, 0:rows, :]
                 + side * y_own[m, h]
             )
-        for copy in out_copies(m):
-            copy.start()
-        return carry
-
-    lax.fori_loop(0, systems, finish, 0)
-
-    def close_out(m, carry):
-        for copy in out_copies(m):
-            copy.wait()
-        return carry
-
-    lax.fori_loop(0, systems, close_out, 0)
-
-    def close_send(offset, carry):
-        send_to(offset).wait_send()
-        return carry
-
-    lax.fori_loop(1, group, close_send, 0)
-    for dz, dy in DIRECTIONS:
-
-        @pl.when(has(dz, dy))
-        def _(dz=dz, dy=dy):
-            label_copy(dz, dy).wait_send()
-            halo_copy(dz, dy).wait_send()
+        for i, (source, target) in enumerate(((out_s, solution_ref), (out_r, residual_ref))):
+            copies.append(pltpu.make_async_copy(source.at[m], target.at[m], out_sem.at[i, m]))
+            copies[-1].start()
+    for copy in copies:
+        copy.wait()
 
 
 def on_device(
@@ -472,21 +528,33 @@
     label_pad = -(-9 * y_blocks // 8) * 8
     f32 = jnp.float32
     vmem = pl.BlockSpec(memory_space=pltpu.VMEM)
-    smem = pl.BlockSpec(memory_space=pltpu.SMEM)
-    hbm = pl.BlockSpec(memory_space=pl.ANY)
+    hbm = pl.BlockSpec(memory_space=pltpu.HBM)
     out = jax.ShapeDtypeStruct((systems,) + right_side.shape, f32)
     dma = pltpu.SemaphoreType.DMA
-    return pl.pallas_call(
+    tall, wide = depth + 2 * REACH, depth + 2
+    fields = pl.pallas_call(
         functools.partial(kernel, grid),
-        out_shape=(out, out),
-        in_specs=[vmem, vmem, smem, smem, smem, smem, vmem],
-        out_specs=(hbm, hbm),
+        out_shape=tuple(
+            jax.ShapeDtypeStruct(shape, f32)
+            for shape in (
+                (halves, tall, ring, lanes),
+                (systems, halves, tall, ring, lanes),
+                (systems, halves, wide, ring, lanes),
+                (systems, halves, wide, ring, lanes),
+                (systems, halves, depth, rows, lanes),
+                (6, systems, lanes),
+            )
+        ),
+        in_specs=[hbm] * 7,
+        out_specs=(vmem,) * 6,
         scratch_shapes=[
-            pltpu.VMEM((halves, depth + 2 * REACH, ring, lanes), f32),
-            pltpu.VMEM((systems, halves, depth + 2 * REACH, ring, lanes), f32),
-            pltpu.VMEM((systems, halves, depth + 2, ring, lanes), f32),
-            pltpu.VMEM((systems, halves, depth + 2, ring, lanes), f32),
-            pltpu.VMEM((systems, halves, depth, rows, lanes), f32),
+            pltpu.VMEM(right_side.shape, f32),
+            pltpu.VMEM(labels.shape, jnp.int32),
+            pltpu.SMEM(region_coeff.shape, f32),
+            pltpu.SMEM(shift_index.shape, jnp.int32),
+            pltpu.SMEM(shift_table.shape, f32),
+            pltpu.SMEM(time_step.shape, f32),
+            pltpu.VMEM(block_inverse.shape, f32),
             pltpu.VMEM((systems, 2 * lanes, 2 * lanes), jnp.bfloat16),
             pltpu.VMEM((label_pad, nx), f32),
             pltpu.VMEM((label_pad, labels.shape[2]), f32),
@@ -499,21 +567,27 @@
             pltpu.VMEM((9,) + labels.shape, jnp.int32),
             pltpu.VMEM((systems, lanes), f32),
             pltpu.VMEM((group, systems, lanes), f32),
-            pltpu.VMEM((6, systems, lanes), f32),
-            pltpu.VMEM(out.shape, f32),
-            pltpu.VMEM(out.shape, f32),
+            dma((7,)),
+            pltpu.SemaphoreType.REGULAR((max(1, max(grid) - 3),)),
             dma((9,)),
             dma((9,)),
             dma((9,)),
             dma((9,)),
             dma((group,)),
             dma((group,)),
-            dma((2, systems)),
         ],
         compiler_params=pltpu.CompilerParams(
-            collective_id=0, has_side_effects=True, vmem_limit_bytes=40 * 1024 * 1024
+            collective_id=0, has_side_effects=True, vmem_limit_bytes=32 * 1024 * 1024
         ),
     )(right_side, labels, region_coeff, shift_index, shift_table, time_step, block_inverse)
+    return pl.pallas_call(
+        finish,
+        out_shape=(out, out),
+        in_specs=[vmem] * 6,
+        out_specs=(hbm, hbm),
+        scratch_shapes=[pltpu.VMEM(out.shape, f32), pltpu.VMEM(out.shape, f32), dma((2, systems))],
+        compiler_params=pltpu.CompilerParams(vmem_limit_bytes=32 * 1024 * 1024),
+    )(*fields)
 
 
 def solution(mesh):

time: 34 us -> 31.6 us (0.929)
  Pallas kernels: 27.2 us -> 25.4 us
  local copies, waits for them, and re-layouts: 5.2 us -> 4.58 us
    pallas_call x1 -> x2, Pallas kernels: 27.2 us -> 25.4 us  [the longest x1 24 us: on_device(): pl.pallas_call(functools.partial(kernel, grid), out_shape=tuple((jax.Shap...]
    unnamed x14 -> x12, local copies, waits for them, and re-layouts: 5.2 us -> 4.58 us
where the time goes in v2:
time: 31.6 us; the launch traced here: 31.3 us
  Pallas kernels  25.4 us (80%)
  local copies, waits for them, and re-layouts  4.58 us (14%)
  between operations  1.3 us (4%)
    pallas_call x1, Pallas kernels, on_device(): pl.pallas_call(functools.partial(kernel, grid), out_shape=tuple((jax.Shap...  24 us
    unnamed x12, local copies, waits for them, and re-layouts  4.58 us
    pallas_call x1, Pallas kernels, on_device(): pl.pallas_call(finish, out_shape=(out, out), in_specs=[vmem] * 6, out_spe...  1.46 us

profile of v2, /device:TPU:0, one launch (start us, length us, event | category | flops | bytes accessed | tf_op | source)
XLA Modules:
  0.0 31.3 jit_solution(13977995250598152450)
XLA Ops:
  1.3 0.0 copy-start
  1.3 1.0 %copy-done = f32[8,128,128]{2,1,0:T(8,128)S(1)} copy-done((f32[8,128,128]{2,1,0:T(8,128)S(1)}, f32[8,128,128]{2,1,0:T(8,128)}, u32[]{:S(2)}) %copy-start) | copy-done | bytes 524312
  2.3 0.0 copy-start.1
  2.3 0.9 %copy-done.1 = f32[8,16,256]{2,1,0:T(8,128)S(1)} copy-done((f32[8,16,256]{2,1,0:T(8,128)S(1)}, f32[8,16,256]{2,1,0:T(8,128)}, u32[]{:S(2)}) %copy-start.1) | copy-done | bytes 131096
  3.2 0.0 copy-start.2
  3.2 0.7 %copy-done.2 = s32[1,2,32]{2,1,0:T(2,128)S(1)} copy-done((s32[1,2,32]{2,1,0:T(2,128)S(1)}, s32[1,2,32]{2,1,0:T(2,128)}, u32[]{:S(2)}) %copy-start.2) | copy-done | bytes 280
  3.9 0.0 copy-start.3
  3.9 0.7 %copy-done.3 = f32[8]{0:T(128)S(1)} copy-done((f32[8]{0:T(128)S(1)}, f32[8]{0:T(128)}, u32[]{:S(2)}) %copy-start.3) | copy-done | bytes 56
  4.6 0.0 copy-start.4
  4.6 0.7 %copy-done.4 = s32[8]{0:T(128)S(1)} copy-done((s32[8]{0:T(128)S(1)}, s32[8]{0:T(128)}, u32[]{:S(2)}) %copy-start.4) | copy-done | bytes 56
  5.2 0.0 copy-start.5
  5.2 0.7 %copy-done.5 = f32[16]{0:T(128)S(1)} copy-done((f32[16]{0:T(128)S(1)}, f32[16]{0:T(128)}, u32[]{:S(2)}) %copy-start.5) | copy-done | bytes 88
  5.9 24.0 %shard_map.86 = (f32[2,12,24,128]{3,2,1,0:T(8,128)S(1)}, f32[8,2,12,24,128]{4,3,2,1,0:T(8,128)S(1)}, f32[8,2,10,24,128]{4,3,2,1,0:T(8,128)S(1)}, f32[8,2,10,24,1...) custom-call(f32[8,16,256]{2,1,0:T(8,128)S(1)} %copy-done.1, ...), custom_call_target="tpu_custom_call" | custom-call | tf_op jit(solution)/shard_map/pallas_call | solution.py:535
  29.9 1.5 %shard_map.87 = (f32[8,8,16,256]{3,2,1,0:T(8,128)}, f32[8,8,16,256]{3,2,1,0:T(8,128)}) custom-call(f32[2,12,24,128]{3,2,1,0:T(8,128)S(1)} %get-tuple-element.8.r_ext, f32[8,2,12,24,128]{4,3,2,1,0:T(8,128)S(1)} %get-tuple-element.9.p_ext, f32[8,2,10,24,128]{4,3,2,1,0:T(8,128)S(1)} %get-tuple-element.10.q_ext, ...), custom_call_target="tpu_custom_call" | custom-call | tf_op jit(solution)/shard_map/pallas_call | solution.py:583
Async XLA Ops:
  1.3 1.0 %copy-start = (f32[8,128,128]{2,1,0:T(8,128)S(1)}, f32[8,128,128]{2,1,0:T(8,128)}, u32[]{:S(2)}) copy-start(f32[8,128,128]{2,1,0:T(8,128)} %inverse_hbm.1) | copy-start | bytes 1572868
  2.3 0.9 %copy-start.1 = (f32[8,16,256]{2,1,0:T(8,128)S(1)}, f32[8,16,256]{2,1,0:T(8,128)}, u32[]{:S(2)}) copy-start(f32[8,16,256]{2,1,0:T(8,128)} %right_hbm.1) | copy-start | bytes 393220
  3.2 0.7 %copy-start.2 = (s32[1,2,32]{2,1,0:T(2,128)S(1)}, s32[1,2,32]{2,1,0:T(2,128)}, u32[]{:S(2)}) copy-start(s32[1,2,32]{2,1,0:T(2,128)} %labels_hbm.1) | copy-start | bytes 772
  3.9 0.7 %copy-start.3 = (f32[8]{0:T(128)S(1)}, f32[8]{0:T(128)}, u32[]{:S(2)}) copy-start(f32[8]{0:T(128)} %coeff_hbm.1) | copy-start | bytes 100
  4.6 0.7 %copy-start.4 = (s32[8]{0:T(128)S(1)}, s32[8]{0:T(128)}, u32[]{:S(2)}) copy-start(s32[8]{0:T(128)} %index_hbm.1) | copy-start | bytes 100
  5.2 0.7 %copy-start.5 = (f32[16]{0:T(128)S(1)}, f32[16]{0:T(128)}, u32[]{:S(2)}) copy-start(f32[16]{0:T(128)} %table_hbm.1) | copy-start | bytes 196

commit v3 on v2

--- a/solution.py
+++ b/solution.py
@@ -579,7 +579,20 @@
         compiler_params=pltpu.CompilerParams(
             collective_id=0, has_side_effects=True, vmem_limit_bytes=32 * 1024 * 1024
         ),
-    )(right_side, labels, region_coeff, shift_index, shift_table, time_step, block_inverse)
+    )(
+        *(
+            x if x is time_step else pltpu.with_memory_space_constraint(x, pltpu.HBM)
+            for x in (
+                right_side,
+                labels,
+                region_coeff,
+                shift_index,
+                shift_table,
+                time_step,
+                block_inverse,
+            )
+        )
+    )
     return pl.pallas_call(
         finish,
         out_shape=(out, out),

time: 31.6 us -> 26.6 us (0.84)
  local copies, waits for them, and re-layouts: 4.58 us -> 0 us
    unnamed x12 -> x0, local copies, waits for them, and re-layouts: 4.58 us -> none
where the time goes in v3:
time: 26.6 us; the launch traced here: 26.4 us
  Pallas kernels  25.1 us (94%)
  between operations  1.29 us (5%)
    pallas_call x1, Pallas kernels, on_device(): pl.pallas_call(functools.partial(kernel, grid), out_shape=tuple((jax.Shap...  23.7 us
    pallas_call x1, Pallas kernels, on_device(): pl.pallas_call(finish, out_shape=(out, out), in_specs=[vmem] * 6, out_spe...  1.46 us

profile of v3, /device:TPU:0, one launch (start us, length us, event | category | flops | bytes accessed | tf_op | source)
XLA Modules:
  0.0 26.4 jit_solution(15764984810428602728)
XLA Ops:
  1.3 23.7 %shard_map.86 = (f32[2,12,24,128]{3,2,1,0:T(8,128)S(1)}, f32[8,2,12,24,128]{4,3,2,1,0:T(8,128)S(1)}, f32[8,2,10,24,128]{4,3,2,1,0:T(8,128)S(1)}, f32[8,2,10,24,1...) custom-call(f32[8,16,256]{2,1,0:T(8,128)} %right_hbm.1, s32[1,2,32]{2,1,0:T(2,128)} %labels_hbm.1, ...), custom_call_target="tpu_custom_call" | custom-call | tf_op jit(solution)/shard_map/pallas_call | solution.py:535
  25.0 1.5 %shard_map.87 = (f32[8,8,16,256]{3,2,1,0:T(8,128)}, f32[8,8,16,256]{3,2,1,0:T(8,128)}) custom-call(f32[2,12,24,128]{3,2,1,0:T(8,128)S(1)} %get-tuple-element.8.r_ext, f32[8,2,12,24,128]{4,3,2,1,0:T(8,128)S(1)} %get-tuple-element.9.p_ext, f32[8,2,10,24,128]{4,3,2,1,0:T(8,128)S(1)} %get-tuple-element.10.q_ext, ...), custom_call_target="tpu_custom_call" | custom-call | tf_op jit(solution)/shard_map/pallas_call | solution.py:596

commit v4 on v3

--- a/solution.py
+++ b/solution.py
@@ -81,6 +81,7 @@
     label_recv,
     message,
     gathered,
+    table,
     load_sem,
     near_sem,
     send_sem,
@@ -249,8 +250,8 @@
 
     label_rows[...] = jnp.zeros_like(label_rows)
     for s in range(9):
-        table = labels_ref[0] if s == slot(0, 0) else label_recv[s, 0]
-        label_rows[s * y_blocks : (s + 1) * y_blocks, :] = table.astype(jnp.float32)
+        near_labels = labels_ref[0] if s == slot(0, 0) else label_recv[s, 0]
+        label_rows[s * y_blocks : (s + 1) * y_blocks, :] = near_labels.astype(jnp.float32)
     spread = jnp.where(
         lax.broadcasted_iota(jnp.int32, (label_cols, nx), 0)
         == lax.broadcasted_iota(jnp.int32, (label_cols, nx), 1) // EDGE,
@@ -408,11 +409,12 @@
             signal_near(near_sem.at[r + 1])
 
     lane = lax.broadcasted_iota(jnp.int32, (systems, lanes), 1)
-    packed = coefs[0]
-    for quantity in range(1, 6):
-        packed = jnp.where(lane == quantity, coefs[quantity], packed)
+    place = lax.broadcasted_iota(jnp.int32, (systems, lanes), 0)
+    packed = jnp.zeros((systems, lanes), jnp.float32)
+    for quantity in range(6):
+        packed = jnp.where(lane == place + quantity * systems, coefs[quantity], packed)
+    packed = jnp.sum(packed, axis=0, keepdims=True)
     message[...] = packed
-    gathered[me] = packed
 
     def gather_copy(device, source):
         return pltpu.make_async_remote_copy(
@@ -448,33 +450,34 @@
 
     lax.fori_loop(1, group, receive_step, 0)
 
-    def column(source, quantity):
-        return jnp.broadcast_to(
-            gathered[source][:, quantity : quantity + 1], (systems, lanes)
-        )
-
-    a_all = [column(d, 0) for d in range(group)]
-    c_all = [column(d, 1) for d in range(group)]
-    rz_0, curvature_0 = sum(a_all), sum(c_all)
-    alpha_0 = rz_0 / curvature_0
-    kept = [1.0 - alpha_0 * column(d, 5) for d in range(group)]
-    g_all = [column(d, 2) for d in range(group)]
-    rz_1 = sum(
-        kept[d] * kept[d] * a_all[d] + alpha_0 * alpha_0 * g_all[d] for d in range(group)
+    gathered[me] = packed
+    for source in range(group):
+        table[source : source + 1, :] = gathered[source]
+
+    def view(rows_of, quantity):
+        return pltpu.roll(rows_of, lanes - quantity * systems, 1) if quantity else rows_of
+
+    def over_devices(x):
+        return jnp.sum(x, axis=0, keepdims=True)
+
+    everyone = table[...]
+    a_all, c_all, g_all, f_all, e_all, sigma_all = (view(everyone, i) for i in range(6))
+    rz_0 = over_devices(a_all)
+    alpha_0 = rz_0 / over_devices(c_all)
+    kept = 1.0 - alpha_0 * sigma_all
+    rz_1 = over_devices(kept * kept * a_all + alpha_0 * alpha_0 * g_all)
+    beta = rz_1 / rz_0
+    k = kept + beta
+    curvature_1 = over_devices(
+        k * k * c_all - alpha_0 * k * (f_all + g_all) + alpha_0 * alpha_0 * e_all
     )
-    beta = rz_1 / rz_0
-    curvature_1 = zero
-    for d in range(group):
-        k = kept[d] + beta
-        curvature_1 = curvature_1 + (
-            k * k * c_all[d]
-            - alpha_0 * k * (column(d, 3) + g_all[d])
-            + alpha_0 * alpha_0 * column(d, 4)
-        )
     alpha_1 = rz_1 / curvature_1
-    own_k = 1.0 - alpha_0 * sigma + beta
-    coefs[0] = alpha_0 + alpha_1 * own_k
-    coefs[1] = alpha_0 * alpha_1
+    own_k = 1.0 - alpha_0 * view(packed, 5) + beta
+    for i, row in enumerate((alpha_0 + alpha_1 * own_k, alpha_0 * alpha_1)):
+        spread_row = jnp.where(lane == place, jnp.broadcast_to(row, (systems, lanes)), 0.0)
+        coefs[i] = jnp.broadcast_to(
+            jnp.sum(spread_row, axis=1, keepdims=True), (systems, lanes)
+        )
 
     def close_send(offset, carry):
         send_to(offset).wait_send()
@@ -565,8 +568,9 @@
             pltpu.VMEM((2, depth, REACH, nx), f32),
             pltpu.VMEM((2, 2, REACH, REACH, nx), f32),
             pltpu.VMEM((9,) + labels.shape, jnp.int32),
-            pltpu.VMEM((systems, lanes), f32),
-            pltpu.VMEM((group, systems, lanes), f32),
+            pltpu.VMEM((1, lanes), f32),
+            pltpu.VMEM((group, 1, lanes), f32),
+            pltpu.VMEM((group, lanes), f32),
             dma((7,)),
             pltpu.SemaphoreType.REGULAR((max(1, max(grid) - 3),)),
             dma((9,)),

time: 26.6 us -> 26.5 us (level)
  no operation moved by 1% of the time
where the time goes in v4:
time: 26.5 us; the launch traced here: 26.3 us
  Pallas kernels  25 us (94%)
  between operations  1.29 us (5%)
    pallas_call x1, Pallas kernels, on_device(): pl.pallas_call(functools.partial(kernel, grid), out_shape=tuple((jax.Shap...  23.6 us
    pallas_call x1, Pallas kernels, on_device(): pl.pallas_call(finish, out_shape=(out, out), in_specs=[vmem] * 6, out_spe...  1.46 us

profile of v4, /device:TPU:0, one launch (start us, length us, event | category | flops | bytes accessed | tf_op | source)
XLA Modules:
  0.0 26.3 jit_solution(6005805375005870513)
XLA Ops:
  1.3 23.6 %shard_map.86 = (f32[2,12,24,128]{3,2,1,0:T(8,128)S(1)}, f32[8,2,12,24,128]{4,3,2,1,0:T(8,128)S(1)}, f32[8,2,10,24,128]{4,3,2,1,0:T(8,128)S(1)}, f32[8,2,10,24,1...) custom-call(f32[8,16,256]{2,1,0:T(8,128)} %right_hbm.1, s32[1,2,32]{2,1,0:T(2,128)} %labels_hbm.1, ...), custom_call_target="tpu_custom_call" | custom-call | tf_op jit(solution)/shard_map/pallas_call | solution.py:538
  24.8 1.5 %shard_map.87 = (f32[8,8,16,256]{3,2,1,0:T(8,128)}, f32[8,8,16,256]{3,2,1,0:T(8,128)}) custom-call(f32[2,12,24,128]{3,2,1,0:T(8,128)S(1)} %get-tuple-element.8.r_ext, f32[8,2,12,24,128]{4,3,2,1,0:T(8,128)S(1)} %get-tuple-element.9.p_ext, f32[8,2,10,24,128]{4,3,2,1,0:T(8,128)S(1)} %get-tuple-element.10.q_ext, ...), custom_call_target="tpu_custom_call" | custom-call | tf_op jit(solution)/shard_map/pallas_call | solution.py:600

commit v5 on v4

--- a/solution.py
+++ b/solution.py
@@ -285,6 +285,10 @@
                 sub < EDGE // 2, row(1, 0), row(-1, y_blocks - 1)
             )
 
+    for h in range(halves):
+        c_planes[3, h] = pltpu.roll(c_planes[1, h], 1, 0)
+        c_planes[4, h] = pltpu.roll(c_planes[1, h], ring - 1, 0)
+
     smooth = [smooth_xy([c_planes[d, h] for h in range(halves)]) for d in range(3)]
     for h in range(halves):
         low, own, high = (smooth[d][h] for d in range(3))
@@ -311,7 +315,14 @@
         for h in range(halves):
             u = (below[h] + here[h]) + (here[h] + above[h])
             if kind == 2:
-                cu = c_planes[1, h] * u
+                twice = u + u
+                before, after = pltpu.roll(u, 1, 0), pltpu.roll(u, ring - 1, 0)
+                u = twice + before + after
+                cu = (
+                    c_planes[1, h] * twice
+                    + c_planes[3, h] * before
+                    + c_planes[4, h] * after
+                )
             else:
                 cu = (
                     c_planes[c_of(z - 1), h] * below[h]
@@ -320,7 +331,8 @@
                 )
             ku.append(u)
             kcu.append(cu)
-        ku, kcu = smooth_xy(ku), smooth_xy(kcu)
+        along = smooth_x if kind == 2 else smooth_xy
+        ku, kcu = along(ku), along(kcu)
         return [
             (diag[kind, h] + shift) * here[h] - c_planes[c_of(z), h] * ku[h] - kcu[h]
             for h in range(halves)
@@ -561,7 +573,7 @@
             pltpu.VMEM((systems, 2 * lanes, 2 * lanes), jnp.bfloat16),
             pltpu.VMEM((label_pad, nx), f32),
             pltpu.VMEM((label_pad, labels.shape[2]), f32),
-            pltpu.VMEM((3, halves, ring, lanes), f32),
+            pltpu.VMEM((5, halves, ring, lanes), f32),
             pltpu.VMEM((5, halves, ring, lanes), f32),
             pltpu.VMEM((2, depth, REACH, nx), f32),
             pltpu.VMEM((2, REACH, rows, nx), f32),

time: 26.5 us -> 26.3 us (level)
  no operation moved by 1% of the time
where the time goes in v5:
time: 26.3 us; the launch traced here: 26.1 us
  Pallas kernels  24.9 us (95%)
  between operations  1.29 us (5%)
    pallas_call x1, Pallas kernels, on_device(): pl.pallas_call(functools.partial(kernel, grid), out_shape=tuple((jax.Shap...  23.4 us
    pallas_call x1, Pallas kernels, on_device(): pl.pallas_call(finish, out_shape=(out, out), in_specs=[vmem] * 6, out_spe...  1.46 us

profile of v5, /device:TPU:0, one launch (start us, length us, event | category | flops | bytes accessed | tf_op | source)
XLA Modules:
  0.0 26.1 jit_solution(15935898097420331689)
XLA Ops:
  1.3 23.4 %shard_map.86 = (f32[2,12,24,128]{3,2,1,0:T(8,128)S(1)}, f32[8,2,12,24,128]{4,3,2,1,0:T(8,128)S(1)}, f32[8,2,10,24,128]{4,3,2,1,0:T(8,128)S(1)}, f32[8,2,10,24,1...) custom-call(f32[8,16,256]{2,1,0:T(8,128)} %right_hbm.1, s32[1,2,32]{2,1,0:T(2,128)} %labels_hbm.1, ...), custom_call_target="tpu_custom_call" | custom-call | tf_op jit(solution)/shard_map/pallas_call | solution.py:550
  24.7 1.5 %shard_map.87 = (f32[8,8,16,256]{3,2,1,0:T(8,128)}, f32[8,8,16,256]{3,2,1,0:T(8,128)}) custom-call(f32[2,12,24,128]{3,2,1,0:T(8,128)S(1)} %get-tuple-element.8.r_ext, f32[8,2,12,24,128]{4,3,2,1,0:T(8,128)S(1)} %get-tuple-element.9.p_ext, f32[8,2,10,24,128]{4,3,2,1,0:T(8,128)S(1)} %get-tuple-element.10.q_ext, ...), custom_call_target="tpu_custom_call" | custom-call | tf_op jit(solution)/shard_map/pallas_call | solution.py:612
